TPU v7x, 128 devices: a whole 4x4x4 slice. The times are simulated.
128 devices in a mesh: replica: 1, data: 128 (over z, y, x, core).
Axes of the slice: x: 4, y: 4, z: 4, core: 2. Of those that a mesh axis runs over, the one named last changes fastest.
Arguments:
- x: bfloat16 [65536, 896], P(('replica', 'data'))
- adapter_id: int32 [65536], P(('replica', 'data'))
- w_gate: bfloat16 [896, 4864], replicated
- w_up: bfloat16 [896, 4864], replicated
- w_down: bfloat16 [4864, 896], replicated
- a_gate: bfloat16 [256, 896, 4], P('data')
- b_gate: bfloat16 [256, 4, 4864], P('data')
- a_up: bfloat16 [256, 896, 4], P('data')
- b_up: bfloat16 [256, 4, 4864], P('data')
- a_down: bfloat16 [256, 4864, 4], P('data')
- b_down: bfloat16 [256, 4, 896], P('data')
- hot_ids: int32 [4], replicated
- hot_a_gate: bfloat16 [4, 896, 4], replicated
- hot_b_gate: bfloat16 [4, 4, 4864], replicated
- hot_a_up: bfloat16 [4, 896, 4], replicated
- hot_b_up: bfloat16 [4, 4, 4864], replicated
- hot_a_down: bfloat16 [4, 4864, 4], replicated
- hot_b_down: bfloat16 [4, 4, 896], replicated
Outputs:
- output: bfloat16 [65536, 896], P(('replica', 'data'))
All inputs are finite; a program needn't handle non-finite values.
Results may differ from a plain program's by a relative error of at most 0.001.
Values are sent between devices in bfloat16 or wider.
A program may use at most 1 GiB of HBM per device.

v0:
```python
import functools

import jax
import jax.numpy as jnp
from jax import lax
from jax.experimental import pallas as pl
from jax.experimental.pallas import tpu as pltpu
from jax.sharding import PartitionSpec as P

LORA_ALPHA = 32
BF = jnp.bfloat16
F32 = jnp.float32
MESH = pl.DeviceIdType.MESH


def dot(a, b):
    return jnp.dot(a, b, preferred_element_type=F32)


def dot_nt(a, b):
    return lax.dot_general(a, b, (((1,), (1,)), ((), ())), preferred_element_type=F32)


def one_hot(mask):
    return jnp.where(mask, 1.0, 0.0).astype(BF)


def layer_kernel(
    sizes,
    hot_ids, ids, x_hbm, wg_hbm, wu_hbm, wd_hbm,
    ag_hbm, bg_hbm, au_hbm, bu_hbm, ad_hbm, bd_hbm,
    hag_hbm, hbg_hbm, hau_hbm, hbu_hbm, had_hbm, hbd_hbm,
    out_ref,
    x_ref, wg_ref, wu_ref, wd_ref,
    ag, bg, au, bu, ad, bd, hag, hbg, hau, hbu, had, hbd,
    at_hot, at_cold, bgu_hot, bgu_cold, adt_hot, adt_cold, bd_hot, bd_cold,
    put_ref, xh_ref, yh_ref, mask_hot, h_ref, xc_ref,
    send_ref, recv_ref, ysend_ref, ret_ref,
    x_sem, small_sem, gu_sem, d_sem, send_sem, recv_sem, ysend_sem, ret_sem,
):
    group, cap, scale, split = sizes
    me = lax.axis_index("data")
    tok, d_model = x_ref.shape
    d_ff = wg_ref.shape[1]
    n_local, rank = ag.shape[0], ag.shape[1]
    n_hot = hag.shape[0]
    k_hot, k_cold = n_hot * rank, n_local * rank
    cold_rows = group * cap
    hot_rows = xh_ref.shape[0]
    tile = 256
    n_tiles = d_ff // tile

    x_copy = pltpu.make_async_copy(x_hbm, x_ref, x_sem)
    x_copy.start()
    small = [
        pltpu.make_async_copy(src, dst, small_sem.at[k])
        for k, (src, dst) in enumerate(
            [(hag_hbm, hag), (hau_hbm, hau), (hbg_hbm, hbg), (hbu_hbm, hbu), (had_hbm, had), (hbd_hbm, hbd),
             (ag_hbm, ag), (au_hbm, au), (bg_hbm, bg), (bu_hbm, bu), (ad_hbm, ad), (bd_hbm, bd)])
    ]
    for copy in small:
        copy.start()

    def gu_copies(n):
        cols = pl.ds(pl.multiple_of(n * tile, tile), tile)
        return (pltpu.make_async_copy(wg_hbm.at[:, cols], wg_ref.at[:, cols], gu_sem.at[0, n]),
                pltpu.make_async_copy(wu_hbm.at[:, cols], wu_ref.at[:, cols], gu_sem.at[1, n]))

    def start_gu(n, _):
        for copy in gu_copies(n):
            copy.start()
        return 0

    lax.fori_loop(0, n_tiles, start_gu, 0)
    d_copy = pltpu.make_async_copy(wd_hbm, wd_ref, d_sem)
    d_copy.start()

    barrier = pltpu.get_barrier_semaphore()

    def greet(k, _):
        peer = lax.rem(me + k, group)
        pl.semaphore_signal(barrier, inc=1, device_id={"data": peer}, device_id_type=MESH)
        return 0

    lax.fori_loop(1, group, greet, 0)

    id_row = ids[...]
    hot_row = id_row == hot_ids[0]
    for j in range(1, n_hot):
        hot_row = jnp.logical_or(hot_row, id_row == hot_ids[j])
    owner = jnp.where(hot_row, -1, id_row // n_local)
    slot = lax.broadcasted_iota(jnp.int32, (cold_rows, tok), 0)
    owned = (slot // cap) == owner
    before = one_hot(lax.broadcasted_iota(jnp.int32, (tok, tok), 0) < lax.broadcasted_iota(jnp.int32, (tok, tok), 1))
    hot_16 = one_hot(jnp.broadcast_to(jnp.where(hot_row, 0, -1), (16, tok)) == 0)
    cold_rank = dot(one_hot(owned), before)
    hot_rank = dot(hot_16, before)[0:1, :]
    pick_cold = one_hot(jnp.logical_and(owned, cold_rank == (slot % cap).astype(F32)))
    hot_pos = jnp.where(hot_row, hot_rank, -1.0)
    pick_hot = one_hot(lax.broadcasted_iota(jnp.int32, (hot_rows, tok), 0).astype(F32) == hot_pos)

    lane_c = lax.broadcasted_iota(jnp.int32, (128, tok), 0)
    local_flag = one_hot(jnp.logical_and(lane_c < 2 * k_cold, (lane_c % k_cold) // rank == id_row % n_local))
    lane_h = lax.broadcasted_iota(jnp.int32, (2 * k_hot, tok), 0)
    which = (lane_h % k_hot) // rank
    hot_of = jnp.full((2 * k_hot, tok), hot_ids[0], jnp.int32)
    for j in range(1, n_hot):
        hot_of = jnp.where(which == j, hot_ids[j], hot_of)
    hot_flag = one_hot(hot_of == id_row)

    x_copy.wait()
    x_all = x_ref[...]
    send_ref[:, :, 0:d_model] = dot(pick_cold, x_all).astype(BF).reshape(group, cap, d_model)
    send_ref[:, :, d_model:] = dot_nt(pick_cold, local_flag).astype(BF).reshape(group, cap, 128)
    recv_ref[pl.ds(me, 1)] = send_ref[pl.ds(me, 1)]

    pl.semaphore_wait(barrier, group - 1)

    def send_x(k, _):
        peer = lax.rem(me + k, group)
        pltpu.make_async_remote_copy(
            send_ref.at[peer], recv_ref.at[me], send_sem, recv_sem,
            device_id={"data": peer}, device_id_type=MESH).start()
        return 0

    lax.fori_loop(1, group, send_x, 0)

    xh_ref[...] = dot(pick_hot, x_all).astype(BF)
    mask_hot[...] = dot_nt(pick_hot, hot_flag).astype(BF)
    put_ref[:, 0:hot_rows] = pick_hot.T
    put_ref[:, hot_rows:] = pick_cold.T

    for copy in small:
        copy.wait()
    at_hot[0:k_hot, :] = hag[...].reshape(k_hot, d_model)
    at_hot[k_hot:, :] = hau[...].reshape(k_hot, d_model)
    at_cold[0:k_cold, :] = ag[...].reshape(k_cold, d_model)
    at_cold[k_cold:, :] = au[...].reshape(k_cold, d_model)
    for ref, g, u, k in ((bgu_hot, hbg, hbu, k_hot), (bgu_cold, bg, bu, k_cold)):
        ref[...] = jnp.zeros_like(ref)
        ref[0, 0:k, :] = g[...].reshape(k, d_ff)
        ref[1, k:2 * k, :] = u[...].reshape(k, d_ff)
    adt_hot[...] = had[...].reshape(k_hot, d_ff)
    adt_cold[...] = ad[...].reshape(k_cold, d_ff)
    bd_hot[...] = hbd[...].reshape(k_hot, d_model)
    bd_cold[...] = bd[...].reshape(k_cold, d_model)

    def expand(rows, at, bgu, mask, base, first):
        low = dot_nt(rows, at[...]).astype(BF) * mask
        m = rows.shape[0]

        def step(n, _):
            cols = pl.ds(pl.multiple_of(n * tile, tile), tile)
            if first:
                for copy in gu_copies(n):
                    copy.wait()
            gate = dot(rows, wg_ref[:, cols]) + (scale * dot(low, bgu[0, :, cols])).astype(BF).astype(F32)
            up = dot(rows, wu_ref[:, cols]) + (scale * dot(low, bgu[1, :, cols])).astype(BF).astype(F32)
            h_ref[base:base + m, cols] = (jax.nn.silu(gate) * up).astype(BF)
            return 0

        lax.fori_loop(0, n_tiles, step, 0)

    def contract(rows, adt, bdm, mask, k, base):
        m = rows.shape[0]
        h = h_ref[base:base + m, :]
        low = dot_nt(h, adt[...]).astype(BF) * mask[:, 0:k]
        parts = []
        for c in range(0, d_model, tile):
            e = min(c + tile, d_model)
            y = dot(h, wd_ref[:, c:e]) + (scale * dot(low, bdm[:, c:e])).astype(BF).astype(F32)
            parts.append((rows[:, c:e].astype(F32) + y).astype(BF))
        return parts

    def hot_part(lo, hi, first):
        rows, mask = xh_ref[lo:hi, :], mask_hot[lo:hi, :]
        expand(rows, at_hot, bgu_hot, mask, lo, first)
        if first:
            d_copy.wait()
        for c, part in enumerate(contract(rows, adt_hot, bd_hot, mask, k_hot, lo)):
            yh_ref[lo:hi, c * tile:c * tile + part.shape[1]] = part

    hot_part(0, split, True)

    pltpu.make_async_remote_copy(
        send_ref.at[pl.ds(0, group - 1)], recv_ref.at[pl.ds(0, group - 1)], send_sem, recv_sem,
        device_id={"data": lax.rem(me + 1, group)}, device_id_type=MESH).wait()
    xc_ref[...] = recv_ref[:, :, 0:d_model].reshape(cold_rows, d_model)
    mask_cold = recv_ref[:, :, d_model:].reshape(cold_rows, 128)[:, 0:2 * k_cold]
    rows_c = xc_ref[...]
    expand(rows_c, at_cold, bgu_cold, mask_cold, hot_rows, False)
    for c, part in enumerate(contract(rows_c, adt_cold, bd_cold, mask_cold, k_cold, hot_rows)):
        ysend_ref[:, :, c * tile:c * tile + part.shape[1]] = part.reshape(group, cap, part.shape[1])
    ret_ref[pl.ds(me, 1)] = ysend_ref[pl.ds(me, 1)]

    def send_y(k, _):
        peer = lax.rem(me + k, group)
        pltpu.make_async_remote_copy(
            ysend_ref.at[peer], ret_ref.at[me], ysend_sem, ret_sem,
            device_id={"data": peer}, device_id_type=MESH).start()
        return 0

    lax.fori_loop(1, group, send_y, 0)

    hot_part(split, hot_rows, False)

    pltpu.make_async_remote_copy(
        ysend_ref.at[pl.ds(0, group - 1)], ret_ref.at[pl.ds(0, group - 1)], ysend_sem, ret_sem,
        device_id={"data": lax.rem(me + 1, group)}, device_id_type=MESH).wait()
    back = ret_ref[...].reshape(cold_rows, d_model)
    out_ref[...] = (dot(put_ref[:, 0:hot_rows], yh_ref[...]) + dot(put_ref[:, hot_rows:], back)).astype(BF)


def solution(mesh):
    group = mesh.shape["data"]
    token_spec = P(("replica", "data"), None)
    store_spec = P("data", None, None)
    full_mat = P(None, None)
    full_set = P(None, None, None)
    in_specs = (token_spec, P(("replica", "data")), full_mat, full_mat, full_mat) + (store_spec,) * 6 + (P(None),) + (full_set,) * 6

    def device_step(x, adapter_id, w_gate, w_up, w_down, a_gate, b_gate, a_up, b_up, a_down, b_down, hot_ids, hot_a_gate, hot_b_gate, hot_a_up, hot_b_up, hot_a_down, hot_b_down):
        tok, d_model = x.shape
        d_ff = w_gate.shape[1]
        n_local, _, rank = a_gate.shape
        n_hot = hot_ids.shape[0]
        cap = tok // (2 * group)
        cold_rows = group * cap
        hot_rows = -(-(tok - group) // 32) * 32
        split = hot_rows // 2
        k_hot, k_cold = n_hot * rank, n_local * rank
        dma = pltpu.SemaphoreType.DMA

        def sets(n):
            return [pltpu.VMEM((n, rank, d_model), BF), pltpu.VMEM((n, rank, d_ff), BF)] * 2 + [
                pltpu.VMEM((n, rank, d_ff), BF), pltpu.VMEM((n, rank, d_model), BF)]

        scratch = [
            pltpu.VMEM((tok, d_model), BF),
            pltpu.VMEM((d_model, d_ff), BF), pltpu.VMEM((d_model, d_ff), BF), pltpu.VMEM((d_ff, d_model), BF),
            *sets(n_local), *sets(n_hot),
            pltpu.VMEM((2 * k_hot, d_model), BF), pltpu.VMEM((2 * k_cold, d_model), BF),
            pltpu.VMEM((2, 2 * k_hot, d_ff), BF), pltpu.VMEM((2, 2 * k_cold, d_ff), BF),
            pltpu.VMEM((k_hot, d_ff), BF), pltpu.VMEM((k_cold, d_ff), BF),
            pltpu.VMEM((k_hot, d_model), BF), pltpu.VMEM((k_cold, d_model), BF),
            pltpu.VMEM((tok, hot_rows + cold_rows), BF),
            pltpu.VMEM((hot_rows, d_model), BF), pltpu.VMEM((hot_rows, d_model), BF),
            pltpu.VMEM((hot_rows, 2 * k_hot), BF),
            pltpu.VMEM((hot_rows + cold_rows, d_ff), BF),
            pltpu.VMEM((cold_rows, d_model), BF),
            pltpu.VMEM((group, cap, d_model + 128), BF), pltpu.VMEM((group, cap, d_model + 128), BF),
            pltpu.VMEM((group, cap, d_model), BF), pltpu.VMEM((group, cap, d_model), BF),
            dma, dma((12,)), dma((2, d_ff // 256)), dma, dma, dma, dma, dma,
        ]
        hbm = pl.BlockSpec(memory_space=pl.ANY)
        kernel = pl.pallas_call(
            functools.partial(layer_kernel, (group, cap, LORA_ALPHA / rank, split)),
            out_shape=jax.ShapeDtypeStruct((tok, d_model), BF),
            in_specs=[pl.BlockSpec(memory_space=pltpu.SMEM), pl.BlockSpec(memory_space=pltpu.VMEM)] + [hbm] * 16,
            out_specs=pl.BlockSpec(memory_space=pltpu.VMEM),
            scratch_shapes=scratch,
            compiler_params=pltpu.CompilerParams(collective_id=0, has_side_effects=True, vmem_limit_bytes=60 * 1024 * 1024),
        )

        def t(a):
            return jnp.swapaxes(a, 1, 2)

        return kernel(hot_ids, adapter_id.reshape(1, tok), x, w_gate, w_up, w_down,
                      t(a_gate), b_gate, t(a_up), b_up, t(a_down), b_down,
                      t(hot_a_gate), hot_b_gate, t(hot_a_up), hot_b_up, t(hot_a_down), hot_b_down)

    return jax.shard_map(device_step, mesh=mesh, in_specs=in_specs, out_specs=token_spec, check_vma=False)
```

profile of v0, /device:TPU:1, one launch (start us, length us, event | category | flops | bytes accessed | tf_op | source)
XLA Modules:
  0.0 58.2 jit_solution(6601713577487379271)
XLA Ops:
  0.0 56.0 %shard_map.172 = bf16[512,896]{1,0:T(8,128)(2,1)} custom-call(s32[4]{0:T(128)} %hot_ids.1, s32[1,512]{1,0:T(1,128)} %bitcast.13, bf16[512,896]{1,0:T(8,128)(2,1)} %x_hbm.1, bf16[896,4864]{1,0:T(8,128)(2,1)} %wg_hbm.1, bf16[896,4864]{1,0:T(8,128)(2,1)} %wu_hbm.1, bf16[4864,896]{1,0:T(8,128)(2,1)} %wd_hbm.1, bf16[2,4,896]{2,1,0:T(4,128)(2,1)} %bitcast.11, ...), custom_call_target="tpu_custom_call" | custom-call | tf_op jit(solution)/shard_map/pallas_call | solution.py:268
  56.0 2.2 %copy.20 = bf16[512,896]{1,0:T(8,128)(2,1)} copy(bf16[512,896]{1,0:T(8,128)(2,1)} %shard_map.172) | data formatting | bytes 1835008
where the time goes:
time: 58.4 us; the launch traced here: 58.2 us
  Pallas kernels  56 us (96%)
  local copies, waits for them, and re-layouts  2.18 us (4%)
    pallas_call x1, Pallas kernels, device_step(): kernel(hot_ids, adapter_id.reshape(1, tok), x, w_gate, w_up, w_down, t(a_...  56 us
    unnamed x1, local copies, waits for them, and re-layouts  2.18 us

commit v1 on v0

v1 whole, which is shorter than its diff:
```python
import functools

import jax
import jax.numpy as jnp
from jax import lax
from jax.experimental import pallas as pl
from jax.experimental.pallas import tpu as pltpu
from jax.sharding import PartitionSpec as P

LORA_ALPHA = 32
BF = jnp.bfloat16
F32 = jnp.float32
MESH = pl.DeviceIdType.MESH


def dot(a, b):
    return jnp.dot(a, b, preferred_element_type=F32)


def dot_nt(a, b):
    return lax.dot_general(a, b, (((1,), (1,)), ((), ())), preferred_element_type=F32)


def one_hot(mask):
    return jnp.where(mask, 1.0, 0.0).astype(BF)


def layer_kernel(
    sizes,
    hid_hbm, id_hbm, x_hbm, wg_hbm, wu_hbm, wd_hbm,
    ag_hbm, bg_hbm, au_hbm, bu_hbm, ad_hbm, bd_hbm,
    hag_hbm, hbg_hbm, hau_hbm, hbu_hbm, had_hbm, hbd_hbm,
    out_ref,
    hot_ids, ids, x_ref, wg_ref, wu_ref, wd_ref,
    ag, bg, au, bu, ad, bd, hag, hbg, hau, hbu, had, hbd,
    at_ref, bgu_ref, bdn_ref,
    put_ref, xh_ref, yh_ref, mask_hot, h_ref, xc_ref,
    send_ref, recv_ref, ysend_ref, ret_ref,
    id_sem, x_sem, small_sem, gu_sem, d_sem, send_sem, recv_sem, ysend_sem, ret_sem,
):
    group, cap, scale, split, half = sizes
    me = lax.axis_index("data")
    tok, d_model = x_ref.shape
    d_ff = wg_ref.shape[1]
    n_local, rank = ag.shape[0], ag.shape[1]
    n_hot = hag.shape[0]
    k_hot, k_cold = n_hot * rank, n_local * rank
    cold_rows = group * cap
    hot_rows = xh_ref.shape[0]
    tile = 256
    n_tiles = d_ff // tile

    id_copies = [pltpu.make_async_copy(id_hbm, ids, id_sem.at[0]), pltpu.make_async_copy(hid_hbm, hot_ids, id_sem.at[1])]
    for copy in id_copies:
        copy.start()
    x_copy = pltpu.make_async_copy(x_hbm, x_ref, x_sem)
    x_copy.start()
    small = [
        pltpu.make_async_copy(src, dst, small_sem.at[k])
        for k, (src, dst) in enumerate(
            [(hag_hbm, hag), (hau_hbm, hau), (hbg_hbm, hbg), (hbu_hbm, hbu), (had_hbm, had), (hbd_hbm, hbd),
             (ag_hbm, ag), (au_hbm, au), (bg_hbm, bg), (bu_hbm, bu), (ad_hbm, ad), (bd_hbm, bd)])
    ]
    for copy in small:
        copy.start()

    gu_copies = []
    for n in range(n_tiles):
        cols = slice(n * tile, (n + 1) * tile)
        gu_copies.append((pltpu.make_async_copy(wg_hbm.at[:, cols], wg_ref.at[:, cols], gu_sem.at[0, n]),
                          pltpu.make_async_copy(wu_hbm.at[:, cols], wu_ref.at[:, cols], gu_sem.at[1, n])))
    for pair in gu_copies:
        for copy in pair:
            copy.start()
    pieces = [(lo, min(lo + 5, n_tiles)) for lo in range(0, n_tiles, 5)]
    d_copy = pltpu.make_async_copy(wd_hbm, wd_ref.at[:, 0:d_model], d_sem)

    barrier = pltpu.get_barrier_semaphore()

    def others():
        for k in range(1, group):
            p = me + k
            yield jnp.where(p >= group, p - group, p)

    for peer in others():
        pl.semaphore_signal(barrier, inc=1, device_id={"data": peer}, device_id_type=MESH)
    for copy in id_copies:
        copy.wait()

    id_row = ids[...]
    hot_row = id_row == hot_ids[0]
    for j in range(1, n_hot):
        hot_row = jnp.logical_or(hot_row, id_row == hot_ids[j])
    owner = jnp.where(hot_row, -1, id_row // n_local)
    slot = lax.broadcasted_iota(jnp.int32, (cold_rows, tok), 0)
    owned = (slot // cap) == owner
    before = one_hot(lax.broadcasted_iota(jnp.int32, (tok, tok), 0) < lax.broadcasted_iota(jnp.int32, (tok, tok), 1))
    hot_16 = one_hot(jnp.broadcast_to(jnp.where(hot_row, 0, -1), (16, tok)) == 0)
    cold_rank = dot(one_hot(owned), before)
    hot_rank = dot(hot_16, before)[0:1, :]
    pick_cold = one_hot(jnp.logical_and(owned, cold_rank == (slot % cap).astype(F32)))
    hot_pos = jnp.where(hot_row, hot_rank, -1.0)
    pick_hot = one_hot(lax.broadcasted_iota(jnp.int32, (hot_rows, tok), 0).astype(F32) == hot_pos)

    lane = lax.broadcasted_iota(jnp.int32, (128, tok), 0) % half
    is_local = jnp.logical_and(lane >= k_hot, lane < k_hot + k_cold)
    local_flag = one_hot(jnp.logical_and(is_local, (lane - k_hot) // rank == id_row % n_local))
    hot_of = jnp.full((128, tok), -1, jnp.int32)
    for j in range(n_hot):
        hot_of = jnp.where(lane // rank == j, hot_ids[j], hot_of)
    hot_flag = one_hot(hot_of == id_row)

    x_copy.wait()
    x_all = x_ref[...]
    send_ref[:, :, 0:d_model] = dot(pick_cold, x_all).astype(BF).reshape(group, cap, d_model)
    send_ref[:, :, d_model:] = dot_nt(pick_cold, local_flag).astype(BF).reshape(group, cap, 128)
    recv_ref[pl.ds(me, 1)] = send_ref[pl.ds(me, 1)]

    pl.semaphore_wait(barrier, group - 1)

    for peer in others():
        pltpu.make_async_remote_copy(
            send_ref.at[peer], recv_ref.at[me], send_sem, recv_sem,
            device_id={"data": peer}, device_id_type=MESH).start()

    xh_ref[...] = dot(pick_hot, x_all).astype(BF)
    mask_hot[...] = dot_nt(pick_hot, hot_flag).astype(BF)
    put_ref[:, 0:hot_rows] = pick_hot.T
    put_ref[:, hot_rows:] = pick_cold.T

    for copy in small:
        copy.wait()
    pad = jnp.zeros((half - k_hot - k_cold, d_model), BF)

    def both(hot, local, width):
        return [hot[...].reshape(k_hot, width), local[...].reshape(k_cold, width)]

    at_ref[...] = jnp.concatenate(both(hag, ag, d_model) + [pad] + both(hau, au, d_model) + [pad], axis=0)
    pad_ff = jnp.zeros((half - k_hot - k_cold, d_ff), BF)
    none_ff = jnp.zeros((half, d_ff), BF)
    bgu_ref[0] = jnp.concatenate(both(hbg, bg, d_ff) + [pad_ff, none_ff], axis=0)
    bgu_ref[1] = jnp.concatenate([none_ff] + both(hbu, bu, d_ff) + [pad_ff], axis=0)
    bdn_ref[...] = jnp.concatenate(both(hbd, bd, d_model) + [pad], axis=0)
    wide = jnp.zeros((128 - k_hot - k_cold, d_ff), BF)
    wd_ref[:, d_model:] = jnp.concatenate(both(had, ad, d_ff) + [wide], axis=0).T

    def expand(rows, mask, base, first):
        low = dot_nt(rows, at_ref[...]).astype(BF) * mask[:, 0:2 * half]
        m = rows.shape[0]
        for n in range(n_tiles):
            cols = slice(n * tile, (n + 1) * tile)
            if first:
                for p, (lo, hi) in enumerate(pieces):
                    if lo == n:
                        for pair in gu_copies[lo:hi]:
                            for copy in pair:
                                copy.wait()
                        if p == 1:
                            d_copy.start()
            gate = dot(rows, wg_ref[:, cols]) + (scale * dot(low, bgu_ref[0, :, cols])).astype(BF).astype(F32)
            up = dot(rows, wu_ref[:, cols]) + (scale * dot(low, bgu_ref[1, :, cols])).astype(BF).astype(F32)
            h_ref[base:base + m, cols] = (jax.nn.silu(gate) * up).astype(BF)

    def contract(rows, mask, base):
        m = rows.shape[0]
        y = dot(h_ref[base:base + m, :], wd_ref[...])
        low = y[:, d_model:d_model + half].astype(BF) * mask[:, 0:half]
        y = y[:, 0:d_model] + (scale * dot(low, bdn_ref[...])).astype(BF).astype(F32)
        return (rows.astype(F32) + y).astype(BF)

    def hot_part(lo, hi, first):
        rows, mask = xh_ref[lo:hi, :], mask_hot[lo:hi, :]
        expand(rows, mask, lo, first)
        if first:
            d_copy.wait()
        yh_ref[lo:hi, :] = contract(rows, mask, lo)

    hot_part(0, split, True)

    pltpu.make_async_remote_copy(
        send_ref.at[pl.ds(0, group - 1)], recv_ref.at[pl.ds(0, group - 1)], send_sem, recv_sem,
        device_id={"data": lax.rem(me + 1, group)}, device_id_type=MESH).wait()
    xc_ref[...] = recv_ref[:, :, 0:d_model].reshape(cold_rows, d_model)
    mask_cold = recv_ref[:, :, d_model:].reshape(cold_rows, 128)
    rows_c = xc_ref[...]
    expand(rows_c, mask_cold, hot_rows, False)
    ysend_ref[...] = contract(rows_c, mask_cold, hot_rows).reshape(group, cap, d_model)
    ret_ref[pl.ds(me, 1)] = ysend_ref[pl.ds(me, 1)]

    for peer in others():
        pltpu.make_async_remote_copy(
            ysend_ref.at[peer], ret_ref.at[me], ysend_sem, ret_sem,
            device_id={"data": peer}, device_id_type=MESH).start()

    hot_part(split, hot_rows, False)

    pltpu.make_async_remote_copy(
        ysend_ref.at[pl.ds(0, group - 1)], ret_ref.at[pl.ds(0, group - 1)], ysend_sem, ret_sem,
        device_id={"data": lax.rem(me + 1, group)}, device_id_type=MESH).wait()
    back = ret_ref[...].reshape(cold_rows, d_model)
    out_ref[...] = (dot(put_ref[:, 0:hot_rows], yh_ref[...]) + dot(put_ref[:, hot_rows:], back)).astype(BF)


def solution(mesh):
    group = mesh.shape["data"]
    token_spec = P(("replica", "data"), None)
    store_spec = P("data", None, None)
    full_mat = P(None, None)
    full_set = P(None, None, None)
    in_specs = (token_spec, P(("replica", "data")), full_mat, full_mat, full_mat) + (store_spec,) * 6 + (P(None),) + (full_set,) * 6

    def device_step(x, adapter_id, w_gate, w_up, w_down, a_gate, b_gate, a_up, b_up, a_down, b_down, hot_ids, hot_a_gate, hot_b_gate, hot_a_up, hot_b_up, hot_a_down, hot_b_down):
        tok, d_model = x.shape
        d_ff = w_gate.shape[1]
        n_local, _, rank = a_gate.shape
        n_hot = hot_ids.shape[0]
        cap = tok // (2 * group)
        cold_rows = group * cap
        hot_rows = -(-(tok - group) // 32) * 32
        split = hot_rows // 2
        half = 32
        dma = pltpu.SemaphoreType.DMA

        def sets(n):
            return [pltpu.VMEM((n, rank, d_model), BF), pltpu.VMEM((n, rank, d_ff), BF)] * 2 + [
                pltpu.VMEM((n, rank, d_ff), BF), pltpu.VMEM((n, rank, d_model), BF)]

        scratch = [
            pltpu.SMEM((n_hot,), jnp.int32), pltpu.VMEM((1, tok), jnp.int32), pltpu.VMEM((tok, d_model), BF),
            pltpu.VMEM((d_model, d_ff), BF), pltpu.VMEM((d_model, d_ff), BF), pltpu.VMEM((d_ff, d_model + 128), BF),
            *sets(n_local), *sets(n_hot),
            pltpu.VMEM((2 * half, d_model), BF), pltpu.VMEM((2, 2 * half, d_ff), BF), pltpu.VMEM((half, d_model), BF),
            pltpu.VMEM((tok, hot_rows + cold_rows), BF),
            pltpu.VMEM((hot_rows, d_model), BF), pltpu.VMEM((hot_rows, d_model), BF),
            pltpu.VMEM((hot_rows, 128), BF),
            pltpu.VMEM((hot_rows + cold_rows, d_ff), BF),
            pltpu.VMEM((cold_rows, d_model), BF),
            pltpu.VMEM((group, cap, d_model + 128), BF), pltpu.VMEM((group, cap, d_model + 128), BF),
            pltpu.VMEM((group, cap, d_model), BF), pltpu.VMEM((group, cap, d_model), BF),
            dma((2,)), dma, dma((12,)), dma((2, d_ff // 256)), dma, dma, dma, dma, dma,
        ]
        hbm = pl.BlockSpec(memory_space=pl.ANY)
        kernel = pl.pallas_call(
            functools.partial(layer_kernel, (group, cap, LORA_ALPHA / rank, split, half)),
            out_shape=pltpu.VMEM((tok, d_model), BF),
            in_specs=[hbm] * 18,
            out_specs=pl.BlockSpec(memory_space=pltpu.VMEM),
            scratch_shapes=scratch,
            compiler_params=pltpu.CompilerParams(collective_id=0, has_side_effects=True, vmem_limit_bytes=60 * 1024 * 1024),
        )

        def t(a):
            return jnp.swapaxes(a, 1, 2)

        return kernel(hot_ids, adapter_id.reshape(1, tok), x, w_gate, w_up, w_down,
                      t(a_gate), b_gate, t(a_up), b_up, t(a_down), b_down,
                      t(hot_a_gate), hot_b_gate, t(hot_a_up), hot_b_up, t(hot_a_down), hot_b_down)

    return jax.shard_map(device_step, mesh=mesh, in_specs=in_specs, out_specs=token_spec, check_vma=False)
```

time: 58.4 us -> 43.2 us (0.74)
  Pallas kernels: 56 us -> 42.2 us
  local copies, waits for them, and re-layouts: 2.18 us -> 0.93 us
    pallas_call x1, Pallas kernels: 56 us -> 42.2 us  [device_step(): kernel(hot_ids, adapter_id.reshape(1, tok), x, w_gate, w_up, w_down, t(a_...]
    unnamed x1, local copies, waits for them, and re-layouts: 2.18 us -> 0.93 us
where the time goes in v1:
time: 43.2 us; the launch traced here: 43.1 us
  Pallas kernels  42.2 us (98%)
  local copies, waits for them, and re-layouts  0.93 us (2%)
    pallas_call x1, Pallas kernels, device_step(): kernel(hot_ids, adapter_id.reshape(1, tok), x, w_gate, w_up, w_down, t(a_...  42.2 us
    unnamed x1, local copies, waits for them, and re-layouts  0.93 us

profile of v1, /device:TPU:1, one launch (start us, length us, event | category | flops | bytes accessed | tf_op | source)
XLA Modules:
  0.0 43.1 jit_solution(975862713302441260)
XLA Ops:
  0.0 42.2 %shard_map.172 = bf16[512,896]{1,0:T(8,128)(2,1)S(1)} custom-call(s32[4]{0:T(128)} %hid_hbm.1, s32[1,512]{1,0:T(1,128)} %bitcast.13, bf16[512,896]{1,0:T(8,128)(2,1)} %x_hbm.1, bf16[896,4864]{1,0:T(8,128)(2,1)} %wg_hbm.1, bf16[896,4864]{1,0:T(8,128)(2,1)} %wu_hbm.1, bf16[4864,896]{1,0:T(8,128)(2,1)} %wd_hbm.1, bf16[2,4,896]{2,1,0:T(4,128)(2,1)} %bitcast.11, ...), custom_call_target="tpu_custom_call" | custom-call | tf_op jit(solution)/shard_map/pallas_call | solution.py:255
  42.2 0.9 %copy.20 = bf16[512,896]{1,0:T(8,128)(2,1)} copy(bf16[512,896]{1,0:T(8,128)(2,1)S(1)} %shard_map.172) | data formatting | bytes 1835008

commit v2 on v1

--- a/solution.py
+++ b/solution.py
@@ -64,16 +64,33 @@
     for copy in small:
         copy.start()
 
-    gu_copies = []
-    for n in range(n_tiles):
-        cols = slice(n * tile, (n + 1) * tile)
-        gu_copies.append((pltpu.make_async_copy(wg_hbm.at[:, cols], wg_ref.at[:, cols], gu_sem.at[0, n]),
-                          pltpu.make_async_copy(wu_hbm.at[:, cols], wu_ref.at[:, cols], gu_sem.at[1, n])))
-    for pair in gu_copies:
-        for copy in pair:
-            copy.start()
     pieces = [(lo, min(lo + 5, n_tiles)) for lo in range(0, n_tiles, 5)]
-    d_copy = pltpu.make_async_copy(wd_hbm, wd_ref.at[:, 0:d_model], d_sem)
+    quarter = d_model // 4
+
+    def gu_piece(p):
+        cols = slice(pieces[p][0] * tile, pieces[p][1] * tile)
+        return cols, ((wg_hbm, wg_ref, gu_sem.at[0, p]), (wu_hbm, wu_ref, gu_sem.at[1, p]))
+
+    def start_gu(p):
+        if p < len(pieces):
+            cols, pair = gu_piece(p)
+            for r in range(4):
+                rows = slice(r * quarter, (r + 1) * quarter)
+                for src, dst, sem in pair:
+                    pltpu.make_async_copy(src.at[rows, cols], dst.at[rows, cols], sem).start()
+
+    def wait_gu(p):
+        cols, pair = gu_piece(p)
+        for src, dst, sem in pair:
+            pltpu.make_async_copy(src.at[:, cols], dst.at[:, cols], sem).wait()
+
+    def start_d():
+        step = d_ff // 4
+        for r in range(4):
+            rows = slice(r * step, (r + 1) * step)
+            pltpu.make_async_copy(wd_hbm.at[rows, :], wd_ref.at[rows, 0:d_model], d_sem).start()
+
+    start_gu(0)
 
     barrier = pltpu.get_barrier_semaphore()
 
@@ -86,6 +103,7 @@
         pl.semaphore_signal(barrier, inc=1, device_id={"data": peer}, device_id_type=MESH)
     for copy in id_copies:
         copy.wait()
+    start_gu(1)
 
     id_row = ids[...]
     hot_row = id_row == hot_ids[0]
@@ -111,22 +129,11 @@
     hot_flag = one_hot(hot_of == id_row)
 
     x_copy.wait()
+    start_gu(2)
     x_all = x_ref[...]
     send_ref[:, :, 0:d_model] = dot(pick_cold, x_all).astype(BF).reshape(group, cap, d_model)
     send_ref[:, :, d_model:] = dot_nt(pick_cold, local_flag).astype(BF).reshape(group, cap, 128)
     recv_ref[pl.ds(me, 1)] = send_ref[pl.ds(me, 1)]
-
-    pl.semaphore_wait(barrier, group - 1)
-
-    for peer in others():
-        pltpu.make_async_remote_copy(
-            send_ref.at[peer], recv_ref.at[me], send_sem, recv_sem,
-            device_id={"data": peer}, device_id_type=MESH).start()
-
-    xh_ref[...] = dot(pick_hot, x_all).astype(BF)
-    mask_hot[...] = dot_nt(pick_hot, hot_flag).astype(BF)
-    put_ref[:, 0:hot_rows] = pick_hot.T
-    put_ref[:, hot_rows:] = pick_cold.T
 
     for copy in small:
         copy.wait()
@@ -144,6 +151,20 @@
     wide = jnp.zeros((128 - k_hot - k_cold, d_ff), BF)
     wd_ref[:, d_model:] = jnp.concatenate(both(had, ad, d_ff) + [wide], axis=0).T
 
+    pl.semaphore_wait(barrier, group - 1)
+    for p in range(3, len(pieces)):
+        start_gu(p)
+
+    for peer in others():
+        pltpu.make_async_remote_copy(
+            send_ref.at[peer], recv_ref.at[me], send_sem, recv_sem,
+            device_id={"data": peer}, device_id_type=MESH).start()
+
+    xh_ref[...] = dot(pick_hot, x_all).astype(BF)
+    mask_hot[...] = dot_nt(pick_hot, hot_flag).astype(BF)
+    put_ref[:, 0:hot_rows] = pick_hot.T
+    put_ref[:, hot_rows:] = pick_cold.T
+
     def expand(rows, mask, base, first):
         low = dot_nt(rows, at_ref[...]).astype(BF) * mask[:, 0:2 * half]
         m = rows.shape[0]
@@ -152,11 +173,9 @@
             if first:
                 for p, (lo, hi) in enumerate(pieces):
                     if lo == n:
-                        for pair in gu_copies[lo:hi]:
-                            for copy in pair:
-                                copy.wait()
-                        if p == 1:
-                            d_copy.start()
+                        wait_gu(p)
+                        if p == min(1, len(pieces) - 1):
+                            start_d()
             gate = dot(rows, wg_ref[:, cols]) + (scale * dot(low, bgu_ref[0, :, cols])).astype(BF).astype(F32)
             up = dot(rows, wu_ref[:, cols]) + (scale * dot(low, bgu_ref[1, :, cols])).astype(BF).astype(F32)
             h_ref[base:base + m, cols] = (jax.nn.silu(gate) * up).astype(BF)
@@ -172,7 +191,7 @@
         rows, mask = xh_ref[lo:hi, :], mask_hot[lo:hi, :]
         expand(rows, mask, lo, first)
         if first:
-            d_copy.wait()
+            pltpu.make_async_copy(wd_hbm, wd_ref.at[:, 0:d_model], d_sem).wait()
         yh_ref[lo:hi, :] = contract(rows, mask, lo)
 
     hot_part(0, split, True)
@@ -193,12 +212,13 @@
             device_id={"data": peer}, device_id_type=MESH).start()
 
     hot_part(split, hot_rows, False)
+    out_ref[...] = dot(put_ref[:, 0:hot_rows], yh_ref[...]).astype(BF)
 
     pltpu.make_async_remote_copy(
         ysend_ref.at[pl.ds(0, group - 1)], ret_ref.at[pl.ds(0, group - 1)], ysend_sem, ret_sem,
         device_id={"data": lax.rem(me + 1, group)}, device_id_type=MESH).wait()
     back = ret_ref[...].reshape(cold_rows, d_model)
-    out_ref[...] = (dot(put_ref[:, 0:hot_rows], yh_ref[...]) + dot(put_ref[:, hot_rows:], back)).astype(BF)
+    out_ref[...] = (out_ref[...].astype(F32) + dot(put_ref[:, hot_rows:], back)).astype(BF)
 
 
 def solution(mesh):
@@ -237,7 +257,7 @@
             pltpu.VMEM((cold_rows, d_model), BF),
             pltpu.VMEM((group, cap, d_model + 128), BF), pltpu.VMEM((group, cap, d_model + 128), BF),
             pltpu.VMEM((group, cap, d_model), BF), pltpu.VMEM((group, cap, d_model), BF),
-            dma((2,)), dma, dma((12,)), dma((2, d_ff // 256)), dma, dma, dma, dma, dma,
+            dma((2,)), dma, dma((12,)), dma((2, -(-d_ff // 1280))), dma, dma, dma, dma, dma,
         ]
         hbm = pl.BlockSpec(memory_space=pl.ANY)
         kernel = pl.pallas_call(

time: 43.2 us -> 40.6 us (0.940)
  Pallas kernels: 42.2 us -> 39.5 us
    pallas_call x1, Pallas kernels: 42.2 us -> 39.5 us  [device_step(): kernel(hot_ids, adapter_id.reshape(1, tok), x, w_gate, w_up, w_down, t(a_...]
where the time goes in v2:
time: 40.6 us; the launch traced here: 40.5 us
  Pallas kernels  39.5 us (97%)
  local copies, waits for them, and re-layouts  0.93 us (2%)
    pallas_call x1, Pallas kernels, device_step(): kernel(hot_ids, adapter_id.reshape(1, tok), x, w_gate, w_up, w_down, t(a_...  39.5 us
    unnamed x1, local copies, waits for them, and re-layouts  0.93 us

profile of v2, /device:TPU:1, one launch (start us, length us, event | category | flops | bytes accessed | tf_op | source)
XLA Modules:
  0.0 40.5 jit_solution(13258826994302955853)
XLA Ops:
  0.0 39.5 %shard_map.172 = bf16[512,896]{1,0:T(8,128)(2,1)S(1)} custom-call(s32[4]{0:T(128)} %hid_hbm.1, s32[1,512]{1,0:T(1,128)} %bitcast.13, bf16[512,896]{1,0:T(8,128)(2,1)} %x_hbm.1, bf16[896,4864]{1,0:T(8,128)(2,1)} %wg_hbm.1, bf16[896,4864]{1,0:T(8,128)(2,1)} %wu_hbm.1, bf16[4864,896]{1,0:T(8,128)(2,1)} %wd_hbm.1, bf16[2,4,896]{2,1,0:T(4,128)(2,1)} %bitcast.11, ...), custom_call_target="tpu_custom_call" | custom-call | tf_op jit(solution)/shard_map/pallas_call | solution.py:275
  39.5 0.9 %copy.20 = bf16[512,896]{1,0:T(8,128)(2,1)} copy(bf16[512,896]{1,0:T(8,128)(2,1)S(1)} %shard_map.172) | data formatting | bytes 1835008

commit v3 on v2

--- a/solution.py
+++ b/solution.py
@@ -90,17 +90,15 @@
             rows = slice(r * step, (r + 1) * step)
             pltpu.make_async_copy(wd_hbm.at[rows, :], wd_ref.at[rows, 0:d_model], d_sem).start()
 
+    barrier = pltpu.get_barrier_semaphore()
+
+    def after(k):
+        p = me + k
+        return jnp.where(p >= group, p - group, p)
+
+    for k in range(1, group):
+        pl.semaphore_signal(barrier, inc=1, device_id={"data": after(k)}, device_id_type=MESH)
     start_gu(0)
-
-    barrier = pltpu.get_barrier_semaphore()
-
-    def others():
-        for k in range(1, group):
-            p = me + k
-            yield jnp.where(p >= group, p - group, p)
-
-    for peer in others():
-        pl.semaphore_signal(barrier, inc=1, device_id={"data": peer}, device_id_type=MESH)
     for copy in id_copies:
         copy.wait()
     start_gu(1)
@@ -109,7 +107,8 @@
     hot_row = id_row == hot_ids[0]
     for j in range(1, n_hot):
         hot_row = jnp.logical_or(hot_row, id_row == hot_ids[j])
-    owner = jnp.where(hot_row, -1, id_row // n_local)
+    owner = id_row // n_local - me
+    owner = jnp.where(hot_row, -1, jnp.where(owner < 0, owner + group, owner))
     slot = lax.broadcasted_iota(jnp.int32, (cold_rows, tok), 0)
     owned = (slot // cap) == owner
     before = one_hot(lax.broadcasted_iota(jnp.int32, (tok, tok), 0) < lax.broadcasted_iota(jnp.int32, (tok, tok), 1))
@@ -129,14 +128,34 @@
     hot_flag = one_hot(hot_of == id_row)
 
     x_copy.wait()
+    for copy in small:
+        copy.wait()
     start_gu(2)
     x_all = x_ref[...]
     send_ref[:, :, 0:d_model] = dot(pick_cold, x_all).astype(BF).reshape(group, cap, d_model)
     send_ref[:, :, d_model:] = dot_nt(pick_cold, local_flag).astype(BF).reshape(group, cap, 128)
-    recv_ref[pl.ds(me, 1)] = send_ref[pl.ds(me, 1)]
-
-    for copy in small:
-        copy.wait()
+    recv_ref[0:1] = send_ref[0:1]
+
+    half_group = group // 2
+
+    def off(stride):
+        a = (me // stride) % 4
+        return jnp.where(a > 2, 4 - a, a)
+
+    far = off(2) + off(8) + off(32) >= 2
+
+    def send_x():
+        pl.semaphore_wait(barrier, group - 1)
+        for k in range(1, group):
+            pltpu.make_async_remote_copy(
+                send_ref.at[k], recv_ref.at[k], send_sem, recv_sem.at[k // half_group],
+                device_id={"data": after(k)}, device_id_type=MESH).start()
+
+    xh_ref[...] = dot(pick_hot, x_all).astype(BF)
+    mask_hot[...] = dot_nt(pick_hot, hot_flag).astype(BF)
+    put_ref[:, 0:hot_rows] = pick_hot.T
+    put_ref[:, hot_rows:] = pick_cold.T
+
     pad = jnp.zeros((half - k_hot - k_cold, d_model), BF)
 
     def both(hot, local, width):
@@ -150,20 +169,6 @@
     bdn_ref[...] = jnp.concatenate(both(hbd, bd, d_model) + [pad], axis=0)
     wide = jnp.zeros((128 - k_hot - k_cold, d_ff), BF)
     wd_ref[:, d_model:] = jnp.concatenate(both(had, ad, d_ff) + [wide], axis=0).T
-
-    pl.semaphore_wait(barrier, group - 1)
-    for p in range(3, len(pieces)):
-        start_gu(p)
-
-    for peer in others():
-        pltpu.make_async_remote_copy(
-            send_ref.at[peer], recv_ref.at[me], send_sem, recv_sem,
-            device_id={"data": peer}, device_id_type=MESH).start()
-
-    xh_ref[...] = dot(pick_hot, x_all).astype(BF)
-    mask_hot[...] = dot_nt(pick_hot, hot_flag).astype(BF)
-    put_ref[:, 0:hot_rows] = pick_hot.T
-    put_ref[:, hot_rows:] = pick_cold.T
 
     def expand(rows, mask, base, first):
         low = dot_nt(rows, at_ref[...]).astype(BF) * mask[:, 0:2 * half]
@@ -174,8 +179,12 @@
                 for p, (lo, hi) in enumerate(pieces):
                     if lo == n:
                         wait_gu(p)
+                        if p == 0:
+                            for q in range(3, len(pieces)):
+                                start_gu(q)
                         if p == min(1, len(pieces) - 1):
                             start_d()
+                            pl.when(far)(send_x)
             gate = dot(rows, wg_ref[:, cols]) + (scale * dot(low, bgu_ref[0, :, cols])).astype(BF).astype(F32)
             up = dot(rows, wu_ref[:, cols]) + (scale * dot(low, bgu_ref[1, :, cols])).astype(BF).astype(F32)
             h_ref[base:base + m, cols] = (jax.nn.silu(gate) * up).astype(BF)
@@ -192,31 +201,40 @@
         expand(rows, mask, lo, first)
         if first:
             pltpu.make_async_copy(wd_hbm, wd_ref.at[:, 0:d_model], d_sem).wait()
+            pl.when(jnp.logical_not(far))(send_x)
         yh_ref[lo:hi, :] = contract(rows, mask, lo)
 
     hot_part(0, split, True)
 
-    pltpu.make_async_remote_copy(
-        send_ref.at[pl.ds(0, group - 1)], recv_ref.at[pl.ds(0, group - 1)], send_sem, recv_sem,
-        device_id={"data": lax.rem(me + 1, group)}, device_id_type=MESH).wait()
-    xc_ref[...] = recv_ref[:, :, 0:d_model].reshape(cold_rows, d_model)
-    mask_cold = recv_ref[:, :, d_model:].reshape(cold_rows, 128)
-    rows_c = xc_ref[...]
-    expand(rows_c, mask_cold, hot_rows, False)
-    ysend_ref[...] = contract(rows_c, mask_cold, hot_rows).reshape(group, cap, d_model)
-    ret_ref[pl.ds(me, 1)] = ysend_ref[pl.ds(me, 1)]
-
-    for peer in others():
+    half_rows = half_group * cap
+    for part in range(2):
+        lo, hi = part * half_group, (part + 1) * half_group
+        first = max(lo, 1)
         pltpu.make_async_remote_copy(
-            ysend_ref.at[peer], ret_ref.at[me], ysend_sem, ret_sem,
-            device_id={"data": peer}, device_id_type=MESH).start()
+            send_ref.at[pl.ds(first, hi - first)], recv_ref.at[pl.ds(first, hi - first)], send_sem, recv_sem.at[part],
+            device_id={"data": after(1)}, device_id_type=MESH).wait_recv()
+        base = part * half_rows
+        xc_ref[base:base + half_rows, :] = recv_ref[lo:hi, :, 0:d_model].reshape(half_rows, d_model)
+        mask_cold = recv_ref[lo:hi, :, d_model:].reshape(half_rows, 128)
+        rows_c = xc_ref[base:base + half_rows, :]
+        expand(rows_c, mask_cold, hot_rows + base, False)
+        ysend_ref[lo:hi] = contract(rows_c, mask_cold, hot_rows + base).reshape(half_group, cap, d_model)
+        if part == 0:
+            ret_ref[0:1] = ysend_ref[0:1]
+        for k in range(first, hi):
+            pltpu.make_async_remote_copy(
+                ysend_ref.at[k], ret_ref.at[k], ysend_sem, ret_sem,
+                device_id={"data": after(group - k)}, device_id_type=MESH).start()
 
     hot_part(split, hot_rows, False)
     out_ref[...] = dot(put_ref[:, 0:hot_rows], yh_ref[...]).astype(BF)
 
     pltpu.make_async_remote_copy(
-        ysend_ref.at[pl.ds(0, group - 1)], ret_ref.at[pl.ds(0, group - 1)], ysend_sem, ret_sem,
-        device_id={"data": lax.rem(me + 1, group)}, device_id_type=MESH).wait()
+        send_ref.at[pl.ds(1, group - 1)], recv_ref.at[pl.ds(1, group - 1)], send_sem, recv_sem.at[0],
+        device_id={"data": after(1)}, device_id_type=MESH).wait_send()
+    pltpu.make_async_remote_copy(
+        ysend_ref.at[pl.ds(1, group - 1)], ret_ref.at[pl.ds(1, group - 1)], ysend_sem, ret_sem,
+        device_id={"data": after(1)}, device_id_type=MESH).wait()
     back = ret_ref[...].reshape(cold_rows, d_model)
     out_ref[...] = (out_ref[...].astype(F32) + dot(put_ref[:, hot_rows:], back)).astype(BF)
 
@@ -257,7 +275,7 @@
             pltpu.VMEM((cold_rows, d_model), BF),
             pltpu.VMEM((group, cap, d_model + 128), BF), pltpu.VMEM((group, cap, d_model + 128), BF),
             pltpu.VMEM((group, cap, d_model), BF), pltpu.VMEM((group, cap, d_model), BF),
-            dma((2,)), dma, dma((12,)), dma((2, -(-d_ff // 1280))), dma, dma, dma, dma, dma,
+            dma((2,)), dma, dma((12,)), dma((2, -(-d_ff // 1280))), dma, dma, dma((2,)), dma, dma,
         ]
         hbm = pl.BlockSpec(memory_space=pl.ANY)
         kernel = pl.pallas_call(

time: 40.6 us -> 39.4 us (0.970)
  Pallas kernels: 39.5 us -> 38.4 us
    pallas_call x1, Pallas kernels: 39.5 us -> 38.4 us  [device_step(): kernel(hot_ids, adapter_id.reshape(1, tok), x, w_gate, w_up, w_down, t(a_...]
where the time goes in v3:
time: 39.4 us; the launch traced here: 39.3 us
  Pallas kernels  38.4 us (97%)
  local copies, waits for them, and re-layouts  0.93 us (2%)
    pallas_call x1, Pallas kernels, device_step(): kernel(hot_ids, adapter_id.reshape(1, tok), x, w_gate, w_up, w_down, t(a_...  38.4 us
    unnamed x1, local copies, waits for them, and re-layouts  0.93 us

profile of v3, /device:TPU:1, one launch (start us, length us, event | category | flops | bytes accessed | tf_op | source)
XLA Modules:
  0.0 39.3 jit_solution(17383824363396852874)
XLA Ops:
  0.0 38.4 %shard_map.172 = bf16[512,896]{1,0:T(8,128)(2,1)S(1)} custom-call(s32[4]{0:T(128)} %hid_hbm.1, s32[1,512]{1,0:T(1,128)} %bitcast.13, bf16[512,896]{1,0:T(8,128)(2,1)} %x_hbm.1, bf16[896,4864]{1,0:T(8,128)(2,1)} %wg_hbm.1, bf16[896,4864]{1,0:T(8,128)(2,1)} %wu_hbm.1, bf16[4864,896]{1,0:T(8,128)(2,1)} %wd_hbm.1, bf16[2,4,896]{2,1,0:T(4,128)(2,1)} %bitcast.11, ...), custom_call_target="tpu_custom_call" | custom-call | tf_op jit(solution)/shard_map/pallas_call | solution.py:293
  38.4 0.9 %copy.20 = bf16[512,896]{1,0:T(8,128)(2,1)} copy(bf16[512,896]{1,0:T(8,128)(2,1)S(1)} %shard_map.172) | data formatting | bytes 1835008
